TPU v7x, 32 devices: a whole 2x2x4 slice. The times are simulated.
32 devices in a mesh: gx: 8 (over y, x, core), gy: 4 (over z).
Axes of the slice: x: 2, y: 2, z: 4, core: 2. Of those that a mesh axis runs over, the one named last changes fastest.
Arguments:
- right_side: float32 [128, 256, 192], P('gx', 'gy'), may hold values from -46 to 46
- diagonal: float32 [128, 256, 192], P('gx', 'gy'), may hold values from 0.1 to 2
Outputs:
- solution_field: float32 [128, 256, 192], P('gx', 'gy')
- residual: float32 [128, 256, 192], P('gx', 'gy')
All inputs are finite; a program needn't handle non-finite values.
Results may differ from a plain program's by a relative error of at most 0.00017.
Values sent between devices are 32-bit elements; how exact they have to be, the bound alone decides.
A program may use at most 64 MiB of HBM per device.

v0:
```python
import jax
import jax.numpy as jnp
from jax import lax
from jax.sharding import PartitionSpec as P

ITERS = 3


def extended(block, sides, width):
    for axis, dim in sides:
        count = lax.axis_size(axis)
        forward = [(i, i + 1) for i in range(count - 1)]
        backward = [(target, source) for source, target in forward]
        low = lax.ppermute(
            lax.slice_in_dim(block, block.shape[dim] - width, None, axis=dim), axis, forward
        )
        high = lax.ppermute(lax.slice_in_dim(block, 0, width, axis=dim), axis, backward)
        block = jnp.concatenate([low, block, high], axis=dim)
    return block


def global_pair(residual, w_now):
    return lax.psum((jnp.sum(residual * residual), jnp.sum(w_now * residual)), ("gx", "gy"))


def trim_rim(field, layers):
    if layers == 0:
        return field
    return field[layers : field.shape[0] - layers, layers : field.shape[1] - layers]


def apply_local(field, diagonal, inside_mask):
    padded = jnp.pad(field, ((0, 0), (0, 0), (1, 1)))
    centre = padded[1:-1, 1:-1, 1:-1]
    beside = padded[2:, 1:-1, 1:-1] + padded[:-2, 1:-1, 1:-1]
    beside = beside + padded[1:-1, 2:, 1:-1] + padded[1:-1, :-2, 1:-1]
    beside = beside + padded[1:-1, 1:-1, 2:] + padded[1:-1, 1:-1, :-2]
    return inside_mask * ((6.0 + diagonal) * centre - beside)


def on_device(right_side, diagonal):
    solution_field = jnp.zeros_like(right_side)
    residual = right_side
    s_field = jnp.zeros_like(right_side)
    p_field = jnp.zeros_like(right_side)
    gamma_prev = jnp.float32(1.0)
    alpha_prev = jnp.float32(1.0)
    rim_depth = ITERS
    block_x = right_side.shape[0]
    block_y = right_side.shape[1]
    stacked = extended(jnp.stack((right_side, diagonal)), (("gx", 1), ("gy", 2)), rim_depth)
    source_pad = stacked[0]
    shift_pad = stacked[1]
    index_x = (
        lax.axis_index("gx") * block_x
        + jnp.arange(block_x + 2 * rim_depth, dtype=jnp.int32)
        - rim_depth
    )
    index_y = (
        lax.axis_index("gy") * block_y
        + jnp.arange(block_y + 2 * rim_depth, dtype=jnp.int32)
        - rim_depth
    )
    inside_x = (index_x >= 0) & (index_x < block_x * lax.axis_size("gx"))
    inside_y = (index_y >= 0) & (index_y < block_y * lax.axis_size("gy"))
    inside_mask = (inside_x[:, None, None] & inside_y[None, :, None]).astype(jnp.float32)
    w_field = apply_local(source_pad, trim_rim(shift_pad, 1), trim_rim(inside_mask, 1))
    z_field = jnp.zeros_like(w_field)
    for step in range(ITERS):
        rim_now = rim_depth - 1 - step
        w_inner = trim_rim(w_field, rim_now)
        gamma, delta = global_pair(residual, w_inner)
        if step == 0:
            beta = jnp.float32(0.0)
            alpha = gamma / delta
        else:
            beta = gamma / gamma_prev
            alpha = gamma / (delta - beta * gamma / alpha_prev)
        s_field = w_inner + beta * s_field
        p_field = residual + beta * p_field
        solution_field = solution_field + alpha * p_field
        residual = residual - alpha * s_field
        if step + 1 < ITERS:
            layers = rim_depth - rim_now + 1
            q_field = apply_local(
                w_field, trim_rim(shift_pad, layers), trim_rim(inside_mask, layers)
            )
            z_field = q_field + beta * trim_rim(z_field, 1)
            w_field = trim_rim(w_field, 1) - alpha * z_field
        gamma_prev = gamma
        alpha_prev = alpha
    return (solution_field, residual)


def solution(mesh):
    placed = (P("gx", "gy", None), P("gx", "gy", None))
    return jax.shard_map(
        on_device,
        mesh=mesh,
        in_specs=placed,
        out_specs=(P("gx", "gy", None), P("gx", "gy", None)),
        check_vma=False,
    )
```

profile of v0, /device:TPU:0, one launch (start us, length us, event | category | flops | bytes accessed | tf_op | source)
XLA Modules:
  0.0 177.2 jit_solution(14748210773020906074)
XLA Ops:
  0.6 0.0 copy-start
  0.6 0.0 copy-start.3
  0.7 2.2 %pad_maximum_fusion.2 = (f32[2,3,64,192]{3,2,1,0:T(8,128)}, f32[2,3,64,192]{3,2,1,0:T(8,128)S(1)}) fusion(f32[1,16,64,192]{3,2,1,0:T(8,128)} %bitcast.15, f32[1,16,64,192]{3,2,1,0:T(8,128)} %bitcast.12), kind=kLoop, calls=%fused_computation.53 | loop fusion | flops 147456 | bytes 2162688 | tf_op jit(solution)/shard_map/slice | solution.py:15
  2.8 2.4 %collective-permute-start = (f32[2,3,64,192]{3,2,1,0:T(8,128)}, f32[2,3,64,192]{3,2,1,0:T(8,128)S(1)}, u32[]{:S(2)}, u32[]{:S(2)}) collective-permute-start(f32[2,3,64,192]{3,2,1,0:T(8,128)} %get-tuple-element.23), channel_id=1, source_target_pairs={{0,4},{4,8},{8,12},{12,16},{16,20},{20,24},{24,28},{1,5},{5,9},{9,... | collective-permute-start | bytes 884744 | tf_op jit(solution)/shard_map/ppermute | solution.py:14
  5.2 1.3 collective-permute-start.1
  6.6 0.1 and_convert_fusion
  6.7 0.1 slice_bitcast_fusion.2
  6.7 0.1 slice_bitcast_fusion.3
  6.8 0.0 collective-permute-done
  6.8 4.1 %collective-permute-done.1 = f32[2,3,64,192]{3,2,1,0:T(8,128)S(1)} collective-permute-done((f32[2,3,64,192]{3,2,1,0:T(8,128)S(1)}, f32[2,3,64,192]{3,2,1,0:T(8,128)S(1)}, u32[]{:S(2)}, u32[]{:S(2)}) %collective-permute-start.1) | collective-permute-done | bytes 294944 | tf_op jit(solution)/shard_map/ppermute | solution.py:17
  10.9 0.0 copy-done
  10.9 0.0 copy-done.3
  10.9 0.1 pad_maximum_fusion.6
  11.0 3.5 %collective-permute-start.2 = (f32[2,22,3,192]{3,2,1,0:T(4,128)S(1)}, f32[2,22,3,192]{3,2,1,0:T(4,128)S(1)}, u32[]{:S(2)}, u32[]{:S(2)}) collective-permute-start(f32[2,22,3,192]{3,2,1,0:T(4,128)S(1)} %get-tuple-element.21), channel_id=1, source_target_pairs={{0,1},{1,2},{2,3},{4,5},{5,6},{6,7},{8,9},{9,10},{10,11},{12,13},{... | collective-permute-start | bytes 304136 | tf_op jit(solution)/shard_map/ppermute | solution.py:14
  14.5 1.3 collective-permute-start.3
  15.8 0.1 slice_bitcast_fusion.4
  15.9 1.6 collective-permute-done.2
  17.5 4.4 %collective-permute-done.3 = f32[2,22,3,192]{3,2,1,0:T(4,128)S(1)} collective-permute-done((f32[2,22,3,192]{3,2,1,0:T(4,128)S(1)}, f32[2,22,3,192]{3,2,1,0:T(4,128)S(1)}, u32[]{:S(2)}, u32[]{:S(2)}) %collective-permute-start.3) | collective-permute-done | bytes 101408 | tf_op jit(solution)/shard_map/ppermute | solution.py:17
  21.9 0.4 pad_maximum_fusion
  22.3 0.2 slice_bitcast_fusion.1
  22.6 0.0 copy-start.2
  22.6 1.8 fusion.3
  24.3 0.0 copy-done.2
  24.4 0.9 multiply_reduce_fusion.4
  25.3 46.8 %all-reduce.5 = (f32[]{:T(128)}, f32[]{:T(128)}) all-reduce(f32[]{:T(128)} %get-tuple-element.7, f32[]{:T(128)} %get-tuple-element.6), channel_id=1, replica_groups=mesh['gx'=8,'gy'=4] {'gx','gy'}, use_global_device_ids=true, to_apply=%region_1.2 | all-reduce | flops 2 | bytes 16 | tf_op jit(solution)/shard_map/psum | solution.py:23
  73.3 0.0 copy-start.1
  73.4 3.7 %multiply_subtract_fusion = (f32[18,66,192]{2,1,0:T(8,128)S(1)}, f32[18,66,192]{2,1,0:T(8,128)}) fusion(f32[20,68,192]{2,1,0:T(8,128)S(1)} %fusion.3, f32[]{:T(128)S(6)} %div.21, f32[22,70,192]{2,1,0:T(8,128)} %copy-done.2, f32[18,66]{1,0:T(8,128)S(1)} %slice_bitcast_fusion.2), kind=kLoop, calls=%fused_computation.25 | loop fusion | flops 2509056 | bytes 10859524 | tf_op jit(solution)/shard_map/sub | solution.py:89
  77.1 2.0 %multiply_reduce_fusion.2 = (f32[]{:T(128)}, f32[]{:T(128)}, f32[16,64,192]{2,1,0:T(8,128)}) fusion(f32[18,66,192]{2,1,0:T(8,128)S(1)} %get-tuple-element.17, f32[16,64,192]{2,1,0:T(8,128)S(1)} %copy-done.1, f32[20,68,192]{2,1,0:T(8,128)S(1)} %fusion.3, f32[]{:T(128)S(6)} %div.21), kind=kLoop, calls=%fused_computation.47 | loop fusion | flops 1179646 | bytes 3145740 | tf_op jit(solution)/shard_map/reduce_sum | solution.py:23
  79.0 40.2 %all-reduce.4 = (f32[]{:T(128)}, f32[]{:T(128)}) all-reduce(f32[]{:T(128)} %get-tuple-element.5, f32[]{:T(128)} %get-tuple-element.4), channel_id=1, replica_groups=mesh['gx'=8,'gy'=4] {'gx','gy'}, use_global_device_ids=true, to_apply=%region_5.6 | all-reduce | flops 2 | bytes 16 | tf_op jit(solution)/shard_map/psum | solution.py:23
  123.5 5.0 %multiply_reduce_fusion = (f32[]{:T(128)}, f32[]{:T(128)}, f32[16,64,192]{2,1,0:T(8,128)}, f32[16,64,192]{2,1,0:T(8,128)}) fusion(f32[18,66,192]{2,1,0:T(8,128)} %get-tuple-element.18, f32[]{:T(128)S(6)} %div.22, f32[18,66,192]{2,1,0:T(8,128)S(1)} %get-tuple-element.17, f32[22,70,192]{2,1,0:T(8,128)} %copy-done.2, f32[16,64]{1,0:T(8,128)S(1)} %slice_bitcast_fusion.4, ...), kind=kLoop, calls=%fused_computation.43 | loop fusion | flops 4128766 | bytes 11558928 | tf_op jit(solution)/shard_map/reduce_sum | solution.py:23
  128.5 40.6 %all-reduce.3 = (f32[]{:T(128)}, f32[]{:T(128)}) all-reduce(f32[]{:T(128)} %get-tuple-element.3, f32[]{:T(128)} %get-tuple-element.2), channel_id=1, replica_groups=mesh['gx'=8,'gy'=4] {'gx','gy'}, use_global_device_ids=true, to_apply=%region_9.10 | all-reduce | flops 2 | bytes 16 | tf_op jit(solution)/shard_map/psum | solution.py:23
  172.9 4.3 %multiply_subtract_fusion.1 = (f32[16,64,192]{2,1,0:T(8,128)}, f32[16,64,192]{2,1,0:T(8,128)}) fusion(f32[16,64,192]{2,1,0:T(8,128)} %get-tuple-element.15, f32[16,64,192]{2,1,0:T(8,128)} %get-tuple-element.14, f32[]{:T(128)S(6)} %div.25, f32[]{:T(128)S(6)} %div.27, f32[20,68,192]{2,1,0:T(8,128)S(1)} %fusion.3, f32[]{:T(128)S(6)} %div.22, ...), kind=kLoop, calls=%fused_computation.41 | loop fusion | flops 2949120 | bytes 6291476 | tf_op jit(solution)/shard_map/sub | solution.py:82
  (3 shorter events, 0.0 us)
Async XLA Ops:
  0.6 10.3 %copy-start = (f32[16,64,192]{2,1,0:T(8,128)S(1)}, f32[16,64,192]{2,1,0:T(8,128)}, u32[]{:S(2)}) copy-start(f32[16,64,192]{2,1,0:T(8,128)} %param.2) | copy-start | bytes 2359300
  0.6 10.3 %copy-start.3 = (f32[16,64,192]{2,1,0:T(8,128)S(1)}, f32[16,64,192]{2,1,0:T(8,128)}, u32[]{:S(2)}) copy-start(f32[16,64,192]{2,1,0:T(8,128)} %param.3) | copy-start | bytes 2359300
  2.8 4.0 %collective-permute-start = (f32[2,3,64,192]{3,2,1,0:T(8,128)}, f32[2,3,64,192]{3,2,1,0:T(8,128)S(1)}, u32[]{:S(2)}, u32[]{:S(2)}) collective-permute-start(f32[2,3,64,192]{3,2,1,0:T(8,128)} %get-tuple-element.23), channel_id=1, source_target_pairs={{0,4},{4,8},{8,12},{12,16},{16,20},{20,24},{24,28},{1,5},{5,9},{9,... | collective-permute-start | bytes 884744 | tf_op jit(solution)/shard_map/ppermute | solution.py:14
  5.2 5.7 %collective-permute-start.1 = (f32[2,3,64,192]{3,2,1,0:T(8,128)S(1)}, f32[2,3,64,192]{3,2,1,0:T(8,128)S(1)}, u32[]{:S(2)}, u32[]{:S(2)}) collective-permute-start(f32[2,3,64,192]{3,2,1,0:T(8,128)S(1)} %get-tuple-element.24), channel_id=1, source_target_pairs={{4,0},{8,4},{12,8},{16,12},{20,16},{24,20},{28,24},{5,1},{9,5},{13... | collective-permute-start | bytes 884744 | tf_op jit(solution)/shard_map/ppermute | solution.py:17
  11.0 6.5 %collective-permute-start.2 = (f32[2,22,3,192]{3,2,1,0:T(4,128)S(1)}, f32[2,22,3,192]{3,2,1,0:T(4,128)S(1)}, u32[]{:S(2)}, u32[]{:S(2)}) collective-permute-start(f32[2,22,3,192]{3,2,1,0:T(4,128)S(1)} %get-tuple-element.21), channel_id=1, source_target_pairs={{0,1},{1,2},{2,3},{4,5},{5,6},{6,7},{8,9},{9,10},{10,11},{12,13},{... | collective-permute-start | bytes 304136 | tf_op jit(solution)/shard_map/ppermute | solution.py:14
  14.5 7.4 %collective-permute-start.3 = (f32[2,22,3,192]{3,2,1,0:T(4,128)S(1)}, f32[2,22,3,192]{3,2,1,0:T(4,128)S(1)}, u32[]{:S(2)}, u32[]{:S(2)}) collective-permute-start(f32[2,22,3,192]{3,2,1,0:T(4,128)S(1)} %get-tuple-element.22), channel_id=1, source_target_pairs={{1,0},{2,1},{3,2},{5,4},{6,5},{7,6},{9,8},{10,9},{11,10},{13,12},{... | collective-permute-start | bytes 304136 | tf_op jit(solution)/shard_map/ppermute | solution.py:17
  22.6 1.8 %copy-start.2 = (f32[22,70,192]{2,1,0:T(8,128)}, f32[22,70,192]{2,1,0:T(8,128)S(1)}, u32[]{:S(2)}) copy-start(f32[22,70,192]{2,1,0:T(8,128)S(1)} %get-tuple-element.19) | copy-start | bytes 3548164
  73.3 3.7 %copy-start.1 = (f32[16,64,192]{2,1,0:T(8,128)S(1)}, f32[16,64,192]{2,1,0:T(8,128)}, u32[]{:S(2)}) copy-start(f32[16,64,192]{2,1,0:T(8,128)} %param.2) | copy-start | bytes 2359300
where the time goes:
time: 178 us; the launch traced here: 177 us
  blocking collectives  128 us (72%)
  other arithmetic  20.3 us (11%)
  waiting for transfers between devices  10.1 us (6%)
  between operations  10.1 us (6%)
  starting transfers between devices  8.48 us (5%)
    psum x3, blocking collectives, global_pair(): lax.psum((jnp.sum(residual * residual), jnp.sum(w_now * residual)), ('gx'...  128 us
    ppermute x2, waiting for transfers between devices, extended(): lax.ppermute(lax.slice_in_dim(block, 0, width, axis=dim), axis, backward)  8.53 us
    reduce_sum x3, other arithmetic, global_pair(): jnp.sum(w_now * residual)  7.87 us
    ppermute x2, starting transfers between devices, extended(): lax.ppermute(lax.slice_in_dim(block, block.shape[dim] - width, None, axis...  5.9 us
    sub x1, other arithmetic, on_device(): residual = residual - alpha * s_field  4.25 us
    sub x1, other arithmetic, on_device(): w_field = trim_rim(w_field, 1) - alpha * z_field  3.7 us
  transfers between devices with their start and end apart: 4, of which 3 were waited for; matrix products, arithmetic and copies ran while one was open for 0% of the time, Pallas kernels for 0%

commit v1 on v0

v1 whole, which is shorter than its diff:
```python
import functools

import jax
import jax.numpy as jnp
from jax import lax
from jax.experimental import pallas as pl
from jax.experimental.pallas import tpu as pltpu
from jax.sharding import PartitionSpec as P

ITERS = 3
SHIFT = 7.0
MESH = pl.DeviceIdType.MESH
DIRS = ((1, 0), (-1, 0), (0, 1), (0, -1), (1, 1), (1, -1), (-1, 1), (-1, -1))
RIM = ITERS
ROWS = 8


def span_x(step, width, size):
    if step == 0:
        return pl.ds(0, size), pl.ds(RIM, size)
    if step > 0:
        return pl.ds(size - width, width), pl.ds(RIM - width, width)
    return pl.ds(0, width), pl.ds(RIM + size, width)


def span_y(step, size):
    if step == 0:
        return pl.ds(0, size), pl.ds(ROWS, size)
    if step > 0:
        return pl.ds(size - ROWS, ROWS), pl.ds(0, ROWS)
    return pl.ds(0, ROWS), pl.ds(ROWS + size, ROWS)


def times_b(field, shift, layer, valid):
    here = field[layer]
    rows, lanes = here.shape
    row0 = jnp.zeros((1, lanes), jnp.float32)
    lane0 = jnp.zeros((rows, 1), jnp.float32)
    beside = field[layer - 1] + field[layer + 1]
    beside = beside + jnp.concatenate([here[1:], row0], 0)
    beside = beside + jnp.concatenate([row0, here[:-1]], 0)
    beside = beside + jnp.concatenate([here[:, 1:], lane0], 1)
    beside = beside + jnp.concatenate([lane0, here[:, :-1]], 1)
    out = (shift[layer] + (6.0 - SHIFT)) * here - beside
    if valid is None:
        return out
    return jnp.where(valid, out, 0.0)


def coefficients(moments):
    def inner(f, g):
        total = None
        for i, a in enumerate(f):
            for j, c in enumerate(g):
                term = a * c * moments[i + j]
                total = term if total is None else total + term
        return total

    def times_a(f):
        out = [SHIFT * f[0]]
        for k in range(1, len(f)):
            out.append(SHIFT * f[k] + f[k - 1])
        return out + [f[-1]]

    def axpy(f, a, g):
        size = max(len(f), len(g))
        out = []
        for k in range(size):
            if k >= len(f):
                out.append(a * g[k])
            elif k >= len(g):
                out.append(f[k])
            else:
                out.append(f[k] + a * g[k])
        return out

    one = jnp.ones_like(moments[0])
    residual, solution_field = [one], []
    s_field, p_field = [], []
    for step in range(ITERS):
        w_field = times_a(residual)
        gamma = inner(residual, residual)
        delta = inner(w_field, residual)
        if step == 0:
            alpha = gamma / delta
            s_field, p_field = w_field, residual
        else:
            beta = gamma / gamma_prev
            alpha = gamma / (delta - beta * gamma / alpha_prev)
            s_field = axpy(w_field, beta, s_field)
            p_field = axpy(residual, beta, p_field)
        solution_field = axpy(solution_field, alpha, p_field)
        residual = axpy(residual, -alpha, s_field)
        gamma_prev, alpha_prev = gamma, alpha
    return solution_field + residual


def kernel(nx, ny, b_ref, d_ref, v1_ref, v2_ref, v3_ref, co_ref,
           v0, dd, v1, v2, part, planes, middle, lines,
           own_sem, send_sem, recv_sem, px_send, px_recv, py_send, py_recv):
    gx, gy = lax.axis_index("gx"), lax.axis_index("gy")
    bx, by, bz = b_ref.shape
    barrier = pltpu.get_barrier_semaphore()

    def there(dx, dy):
        ok = None
        for at, step, count in ((gx, dx, nx), (gy, dy, ny)):
            if step:
                this = (at + step >= 0) & (at + step < count)
                ok = this if ok is None else ok & this
        return ok

    def peer_x(k):
        return lax.rem(gx + k, nx)

    def peer_y(k):
        return lax.rem(gy + k, ny)

    for dx, dy in DIRS[4:]:
        @pl.when(there(dx, dy))
        def _(dx=dx, dy=dy):
            pl.semaphore_signal(barrier, inc=1, device_id=(gx + dx, gy + dy), device_id_type=MESH)

    @pl.loop(1, nx)
    def _(k):
        pl.semaphore_signal(barrier, inc=1, device_id=(peer_x(k), gy), device_id_type=MESH)

    @pl.loop(1, ny)
    def _(k):
        pl.semaphore_signal(barrier, inc=1, device_id=(gx, peer_y(k)), device_id_type=MESH)

    own = []
    for n, (src, dst) in enumerate(((b_ref, v0), (d_ref, dd))):
        own.append(pltpu.make_async_copy(
            src, dst.at[pl.ds(RIM, bx), pl.ds(ROWS, by), :], own_sem.at[n]))
        own[-1].start()

    @pl.when(gx == 0)
    def _():
        v0[0:RIM] = jnp.zeros((RIM,) + v0.shape[1:], jnp.float32)

    @pl.when(gx == nx - 1)
    def _():
        v0[RIM + bx:] = jnp.zeros((RIM,) + v0.shape[1:], jnp.float32)

    @pl.when(gy == 0)
    def _():
        v0[:, 0:ROWS] = jnp.zeros((v0.shape[0], ROWS, bz), jnp.float32)

    @pl.when(gy == ny - 1)
    def _():
        v0[:, ROWS + by:] = jnp.zeros((v0.shape[0], ROWS, bz), jnp.float32)

    expected = nx - 1 + ny - 1
    for dx, dy in DIRS[4:]:
        expected = expected + there(dx, dy).astype(jnp.int32)
    pl.semaphore_wait(barrier, expected)

    def halo(n, dx, dy):
        width = (RIM, RIM - 1)[n] if dy == 0 else (RIM - 1, RIM - 2)[n]
        src, dst = ((b_ref, v0), (d_ref, dd))[n]
        from_x, to_x = span_x(dx, width, bx)
        from_y, to_y = span_y(dy, by)
        index = DIRS.index((dx, dy))
        return pltpu.make_async_remote_copy(
            src_ref=src.at[from_x, from_y, :],
            dst_ref=dst.at[to_x, to_y, :],
            send_sem=send_sem.at[n, index],
            recv_sem=recv_sem.at[n, index],
            device_id=(gx + dx, gy + dy),
            device_id_type=MESH,
        )

    for n in range(2):
        for dx, dy in DIRS:
            @pl.when(there(dx, dy))
            def _(n=n, dx=dx, dy=dy):
                halo(n, dx, dy).start()

    for copy in own:
        copy.wait()
    for n in range(2):
        for dx, dy in DIRS:
            @pl.when(there(-dx, -dy))
            def _(n=n, dx=dx, dy=dy):
                halo(n, dx, dy).wait_recv()

    row = lax.broadcasted_iota(jnp.int32, (by + 2 * ROWS, bz), 0)
    inside_y = ((row >= ROWS) | (gy > 0)) & ((row < ROWS + by) | (gy < ny - 1))

    def inside(layer):
        ok = ((layer >= RIM) | (gx > 0)) & ((layer < RIM + bx) | (gx < nx - 1))
        return inside_y & ok

    inner = slice(ROWS, ROWS + by)

    @pl.loop(1, 2 * RIM + bx - 1)
    def _(layer):
        v1[layer] = times_b(v0, dd, layer, inside(layer))

    @pl.loop(2, 2 * RIM + bx - 2)
    def _(layer):
        v2[layer] = times_b(v1, dd, layer, inside(layer))

    def tile(a):
        whole = jnp.sum(a.reshape(by // 8, 8, bz), 0)
        pad = jnp.concatenate([whole[:, 128:], jnp.zeros((8, 256 - bz), jnp.float32)], 1)
        return whole[:, :128] + pad

    def body(k, sums):
        layer = k + RIM
        f0 = v0[layer, inner]
        f1 = v1[layer, inner]
        f2 = v2[layer, inner]
        f3 = times_b(v2, dd, layer, None)[inner]
        v1_ref[k] = f1
        v2_ref[k] = f2
        v3_ref[k] = f3
        pairs = (f0 * f0, f0 * f1, f1 * f1, f1 * f2, f2 * f2, f2 * f3)
        return tuple(s + jnp.sum(p.reshape(by // 8, 8, bz), 0) for s, p in zip(sums, pairs))

    sums = lax.fori_loop(0, bx, body, (jnp.zeros((8, bz), jnp.float32),) * 6)
    lane = [jnp.sum(jnp.sum(s, 1, keepdims=True), 0, keepdims=True) for s in sums]
    row8 = lax.broadcasted_iota(jnp.int32, (8, 128), 0)
    packed = jnp.zeros((8, 128), jnp.float32)
    for k, s in enumerate(lane):
        packed = jnp.where(row8 == k, s, packed)
    part[...] = packed

    def share(src, slots, k, axis):
        if axis == 0:
            mine, target = gx, (peer_x(k), gy)
            theirs, sems = lax.rem(gx + nx - k, nx), (px_send, px_recv)
        else:
            mine, target = gy, (gx, peer_y(k))
            theirs, sems = lax.rem(gy + ny - k, ny), (py_send, py_recv)
        return pltpu.make_async_remote_copy(
            src_ref=src, dst_ref=slots.at[mine], send_sem=sems[0].at[k - 1],
            recv_sem=sems[1].at[k - 1], device_id=target, device_id_type=MESH)

    def all_sum(src, slots, count, axis):
        mine = gx if axis == 0 else gy

        @pl.loop(1, count)
        def _(k):
            share(src, slots, k, axis).start()

        slots[mine] = src[...]

        @pl.loop(1, count)
        def _(k):
            share(src, slots, k, axis).wait()

        return lax.fori_loop(1, count, lambda k, t: t + slots[k], slots[0])

    middle[...] = all_sum(part, planes, nx, 0)
    total = all_sum(middle, lines, ny, 1)
    moments = [total[k:k + 1] for k in range(6)]
    co = jnp.zeros((8, 128), jnp.float32)
    for k, c in enumerate(coefficients(moments)):
        co = jnp.where(row8 == k, c, co)
    co_ref[...] = co

    for n in range(2):
        for dx, dy in DIRS:
            @pl.when(there(dx, dy))
            def _(n=n, dx=dx, dy=dy):
                halo(n, dx, dy).wait_send()


def on_device(nx, ny, right_side, diagonal):
    bx, by, bz = right_side.shape
    block = jax.ShapeDtypeStruct((bx, by, bz), jnp.float32)
    big = pltpu.VMEM((bx + 2 * RIM, by + 2 * ROWS, bz), jnp.float32)
    vmem = pl.BlockSpec(memory_space=pltpu.VMEM)
    dma = pltpu.SemaphoreType.DMA
    f1, f2, f3, co = pl.pallas_call(
        functools.partial(kernel, nx, ny),
        out_shape=(block, block, block, jax.ShapeDtypeStruct((8, 128), jnp.float32)),
        in_specs=[pl.BlockSpec(memory_space=pl.ANY)] * 2,
        out_specs=(vmem,) * 4,
        scratch_shapes=[
            big, big, big, big,
            pltpu.VMEM((8, 128), jnp.float32),
            pltpu.VMEM((nx, 8, 128), jnp.float32),
            pltpu.VMEM((8, 128), jnp.float32),
            pltpu.VMEM((ny, 8, 128), jnp.float32),
            dma((2,)), dma((2, 8)), dma((2, 8)),
            dma((nx - 1,)), dma((nx - 1,)), dma((ny - 1,)), dma((ny - 1,)),
        ],
        compiler_params=pltpu.CompilerParams(collective_id=0, has_side_effects=True),
    )(right_side, diagonal)
    c = [co[k, 0] for k in range(7)]
    solution_field = c[0] * right_side + c[1] * f1 + c[2] * f2
    residual = c[3] * right_side + c[4] * f1 + c[5] * f2 + c[6] * f3
    return solution_field, residual


def solution(mesh):
    placed = (P("gx", "gy", None), P("gx", "gy", None))
    return jax.shard_map(
        functools.partial(on_device, mesh.shape["gx"], mesh.shape["gy"]),
        mesh=mesh,
        in_specs=placed,
        out_specs=placed,
        check_vma=False,
    )
```

time: 178 us -> 40.5 us (0.23)
  blocking collectives: 128 us -> 0 us
  Pallas kernels: 0 us -> 30.4 us
  other arithmetic: 20.3 us -> 7.96 us
  waiting for transfers between devices: 10.1 us -> 0 us
  between operations: 10.1 us -> 0.65 us
  starting transfers between devices: 8.48 us -> 0 us
    psum x3 -> x0, blocking collectives: 128 us -> none  [global_pair(): lax.psum((jnp.sum(residual * residual), jnp.sum(w_now * residual)), ('gx'...]
    pallas_call x0 -> x1, Pallas kernels: none -> 30.4 us  [on_device(): pl.pallas_call(functools.partial(kernel, nx, ny), out_shape=(block, block...]
    ppermute x4 -> x0, waiting for transfers between devices: 10.1 us -> none  [the longest x2 8.53 us: extended(): lax.ppermute(lax.slice_in_dim(block, 0, width, axis=dim), axis, backward)]
    ppermute x4 -> x0, starting transfers between devices: 8.48 us -> none  [the longest x2 5.9 us: extended(): lax.ppermute(lax.slice_in_dim(block, block.shape[dim] - width, None, axis...]
    add x0 -> x1, other arithmetic: none -> 7.96 us  [on_device(): residual = c[3] * right_side + c[4] * f1 + c[5] * f2 + c[6] * f3]
    sub x2 -> x0, other arithmetic: 7.95 us -> none  [the longest x1 4.25 us: on_device(): residual = residual - alpha * s_field]
    reduce_sum x3 -> x0, other arithmetic: 7.87 us -> none  [global_pair(): jnp.sum(w_now * residual)]
    slice x2 -> x0, other arithmetic: 2.24 us -> none  [extended(): lax.slice_in_dim(block, block.shape[dim] - width, None, axis=dim)]
  transfers between devices with their start and end apart: 4 -> 0, of which waited for: 3 -> 0; matrix products, arithmetic and copies ran while one was open for 0% -> 0% of each run, Pallas kernels for 0% -> 0%
where the time goes in v1:
time: 40.5 us; the launch traced here: 40.3 us
  Pallas kernels  30.4 us (75%)
  other arithmetic  7.96 us (20%)
  local copies, waits for them, and re-layouts  1.25 us (3%)
  between operations  0.65 us (2%)
    pallas_call x1, Pallas kernels, on_device(): pl.pallas_call(functools.partial(kernel, nx, ny), out_shape=(block, block...  30.4 us
    add x1, other arithmetic, on_device(): residual = c[3] * right_side + c[4] * f1 + c[5] * f2 + c[6] * f3  7.96 us

profile of v1, /device:TPU:0, one launch (start us, length us, event | category | flops | bytes accessed | tf_op | source)
XLA Modules:
  0.0 40.3 jit_solution(1375131662281594639)
XLA Ops:
  0.6 0.0 copy-start
  0.6 30.4 %shard_map.41 = (f32[16,64,192]{2,1,0:T(8,128)}, f32[16,64,192]{2,1,0:T(8,128)}, f32[16,64,192]{2,1,0:T(8,128)}, f32[8,128]{1,0:T(8,128)}) custom-call(f32[16,64,192]{2,1,0:T(8,128)} %b_ref.1, f32[16,64,192]{2,1,0:T(8,128)} %d_ref.1), custom_call_target="tpu_custom_call" | custom-call | tf_op jit(solution)/shard_map/pallas_call | solution.py:277
  31.1 0.0 copy-start.1
  31.1 0.7 %copy-done.1 = f32[8,128]{1,0:T(8,128)S(1)} copy-done((f32[8,128]{1,0:T(8,128)S(1)}, f32[8,128]{1,0:T(8,128)}, u32[]{:S(2)}) %copy-start.1) | copy-done | bytes 4120
  31.7 0.6 %fusion = (f32[1,1]{1,0:T(1,128)}, f32[1,1]{1,0:T(1,128)}, f32[1,1]{1,0:T(1,128)}, f32[1,1]{1,0:T(1,128)}, f32[1,1]{1,0:T(1,128)}, /*index=5*/f32[1,1]{1,0:T(1,128)}, f32[1,1]{1,0:T(1,128)}) fusion(f32[8,128]{1,0:T(8,128)S(1)} %copy-done.1), kind=kLoop, calls=%fused_computation.2 | loop fusion | bytes 56 | tf_op jit(solution)/shard_map/slice | solution.py:293
  32.3 0.0 copy-done
  32.3 8.0 %multiply_add_fusion = (f32[16,64,192]{2,1,0:T(8,128)}, f32[16,64,192]{2,1,0:T(8,128)}) fusion(f32[16,64,192]{2,1,0:T(8,128)} %get-tuple-element.9, f32[16,64,192]{2,1,0:T(8,128)} %get-tuple-element.8, f32[16,64,192]{2,1,0:T(8,128)} %get-tuple-element.7, f32[16,64,192]{2,1,0:T(8,128)S(1)} %copy-done, f32[]{:T(128)} %bitcast.6, f32[]{:T(128)} %bitcast.5, ...), kind=kLoop, calls=%fused_computation | loop fusion | flops 2359296 | bytes 4718620 | tf_op jit(solution)/shard_map/add | solution.py:295
Async XLA Ops:
  0.6 31.7 %copy-start = (f32[16,64,192]{2,1,0:T(8,128)S(1)}, f32[16,64,192]{2,1,0:T(8,128)}, u32[]{:S(2)}) copy-start(f32[16,64,192]{2,1,0:T(8,128)} %b_ref.1) | copy-start | bytes 2359300
  31.1 0.7 %copy-start.1 = (f32[8,128]{1,0:T(8,128)S(1)}, f32[8,128]{1,0:T(8,128)}, u32[]{:S(2)}) copy-start(f32[8,128]{1,0:T(8,128)} %get-tuple-element.6) | copy-start | bytes 12292

commit v2 on v1

--- a/solution.py
+++ b/solution.py
@@ -23,12 +23,12 @@
     return pl.ds(0, width), pl.ds(RIM + size, width)
 
 
-def span_y(step, size):
+def span_y(step, width, size):
     if step == 0:
         return pl.ds(0, size), pl.ds(ROWS, size)
     if step > 0:
-        return pl.ds(size - ROWS, ROWS), pl.ds(0, ROWS)
-    return pl.ds(0, ROWS), pl.ds(ROWS + size, ROWS)
+        return pl.ds(size - width, width), pl.ds(ROWS - width, width)
+    return pl.ds(0, width), pl.ds(ROWS + size, width)
 
 
 def times_b(field, shift, layer, valid):
@@ -157,10 +157,11 @@
     pl.semaphore_wait(barrier, expected)
 
     def halo(n, dx, dy):
-        width = (RIM, RIM - 1)[n] if dy == 0 else (RIM - 1, RIM - 2)[n]
+        width = RIM - n if dx == 0 or dy == 0 else RIM - 1 - n
+        width_y = width
         src, dst = ((b_ref, v0), (d_ref, dd))[n]
         from_x, to_x = span_x(dx, width, bx)
-        from_y, to_y = span_y(dy, by)
+        from_y, to_y = span_y(dy, width_y, by)
         index = DIRS.index((dx, dy))
         return pltpu.make_async_remote_copy(
             src_ref=src.at[from_x, from_y, :],
@@ -268,6 +269,28 @@
                 halo(n, dx, dy).wait_send()
 
 
+def combine(f0_ref, f1_ref, f2_ref, f3_ref, co_ref, x_ref, r_ref, x_out, r_out, sems):
+    c = [co_ref[k:k + 1, 0:1] for k in range(7)]
+    count = x_out.shape[0]
+
+    def copy(n, k):
+        src, dst = ((x_out, x_ref), (r_out, r_ref))[n]
+        return pltpu.make_async_copy(src.at[pl.ds(k, 1)], dst.at[pl.ds(k, 1)], sems.at[n, k])
+
+    @pl.loop(0, count)
+    def _(k):
+        f0, f1, f2, f3 = f0_ref[k], f1_ref[k], f2_ref[k], f3_ref[k]
+        x_out[k] = c[0] * f0 + c[1] * f1 + c[2] * f2
+        r_out[k] = c[3] * f0 + c[4] * f1 + c[5] * f2 + c[6] * f3
+        for n in range(2):
+            copy(n, k).start()
+
+    @pl.loop(0, count)
+    def _(k):
+        for n in range(2):
+            copy(n, k).wait()
+
+
 def on_device(nx, ny, right_side, diagonal):
     bx, by, bz = right_side.shape
     block = jax.ShapeDtypeStruct((bx, by, bz), jnp.float32)
@@ -277,7 +300,7 @@
     f1, f2, f3, co = pl.pallas_call(
         functools.partial(kernel, nx, ny),
         out_shape=(block, block, block, jax.ShapeDtypeStruct((8, 128), jnp.float32)),
-        in_specs=[pl.BlockSpec(memory_space=pl.ANY)] * 2,
+        in_specs=[pl.BlockSpec(memory_space=pltpu.HBM)] * 2,
         out_specs=(vmem,) * 4,
         scratch_shapes=[
             big, big, big, big,
@@ -288,12 +311,21 @@
             dma((2,)), dma((2, 8)), dma((2, 8)),
             dma((nx - 1,)), dma((nx - 1,)), dma((ny - 1,)), dma((ny - 1,)),
         ],
-        compiler_params=pltpu.CompilerParams(collective_id=0, has_side_effects=True),
-    )(right_side, diagonal)
-    c = [co[k, 0] for k in range(7)]
-    solution_field = c[0] * right_side + c[1] * f1 + c[2] * f2
-    residual = c[3] * right_side + c[4] * f1 + c[5] * f2 + c[6] * f3
-    return solution_field, residual
+        compiler_params=pltpu.CompilerParams(
+            collective_id=0, has_side_effects=True, vmem_limit_bytes=24 * 2**20),
+    )(*(pltpu.with_memory_space_constraint(a, pltpu.HBM) for a in (right_side, diagonal)))
+    return pl.pallas_call(
+        combine,
+        out_shape=(block, block),
+        in_specs=[vmem] * 5,
+        out_specs=(pl.BlockSpec(memory_space=pl.ANY),) * 2,
+        scratch_shapes=[
+            pltpu.VMEM((bx, by, bz), jnp.float32),
+            pltpu.VMEM((bx, by, bz), jnp.float32),
+            dma((2, bx)),
+        ],
+        compiler_params=pltpu.CompilerParams(vmem_limit_bytes=24 * 2**20),
+    )(right_side, f1, f2, f3, co)
 
 
 def solution(mesh):

time: 40.5 us -> 30.7 us (0.76)
  other arithmetic: 7.96 us -> 0 us
  local copies, waits for them, and re-layouts: 1.25 us -> 0.01 us
  Pallas kernels: 30.4 us -> 29.9 us
    add x1 -> x0, other arithmetic: 7.96 us -> none  [on_device(): residual = c[3] * right_side + c[4] * f1 + c[5] * f2 + c[6] * f3]
    pallas_call x1, Pallas kernels: 30.4 us -> 27.9 us  [on_device(): pl.pallas_call(functools.partial(kernel, nx, ny), out_shape=(block, block...]
    pallas_call x0 -> x1, Pallas kernels: none -> 2.03 us  [on_device(): pl.pallas_call(combine, out_shape=(block, block), in_specs=[vmem] * 5, ou...]
    unnamed x4 -> x2, local copies, waits for them, and re-layouts: 0.66 us -> 0.01 us
    slice x1 -> x0, local copies, waits for them, and re-layouts: 0.59 us -> none  [on_device(): c = [co[k, 0] for k in range(7)]]
where the time goes in v2:
time: 30.7 us; the launch traced here: 30.6 us
  Pallas kernels  29.9 us (97%)
  between operations  0.65 us (2%)
    pallas_call x1, Pallas kernels, on_device(): pl.pallas_call(functools.partial(kernel, nx, ny), out_shape=(block, block...  27.9 us
    pallas_call x1, Pallas kernels, on_device(): pl.pallas_call(combine, out_shape=(block, block), in_specs=[vmem] * 5, ou...  2.03 us

profile of v2, /device:TPU:0, one launch (start us, length us, event | category | flops | bytes accessed | tf_op | source)
XLA Modules:
  0.0 30.6 jit_solution(15143696833725484055)
XLA Ops:
  0.6 0.0 copy-start
  0.6 27.9 %shard_map.41 = (f32[16,64,192]{2,1,0:T(8,128)S(1)}, f32[16,64,192]{2,1,0:T(8,128)S(1)}, f32[16,64,192]{2,1,0:T(8,128)S(1)}, f32[8,128]{1,0:T(8,128)S(1)}) custom-call(f32[16,64,192]{2,1,0:T(8,128)} %f0_ref.1, f32[16,64,192]{2,1,0:T(8,128)} %d_ref.1), custom_call_target="tpu_custom_call" | custom-call | tf_op jit(solution)/shard_map/pallas_call | solution.py:300
  28.5 0.0 copy-done
  28.6 2.0 %shard_map.42 = (f32[16,64,192]{2,1,0:T(8,128)}, f32[16,64,192]{2,1,0:T(8,128)}) custom-call(f32[16,64,192]{2,1,0:T(8,128)S(1)} %copy-done, f32[16,64,192]{2,1,0:T(8,128)S(1)} %get-tuple-element.6.f1_ref, f32[16,64,192]{2,1,0:T(8,128)S(1)} %get-tuple-element.7.f2_ref, f32[16,64,192]{2,1,0:T(8,128)S(1)} %get-tuple-element.8.f3_ref, ...), custom_call_target="tpu_custom_call" | custom-call | tf_op jit(solution)/shard_map/pallas_call | solution.py:317
Async XLA Ops:
  0.6 27.9 %copy-start = (f32[16,64,192]{2,1,0:T(8,128)S(1)}, f32[16,64,192]{2,1,0:T(8,128)}, u32[]{:S(2)}) copy-start(f32[16,64,192]{2,1,0:T(8,128)} %f0_ref.1) | copy-start | bytes 2359300

commit v3 on v2

--- a/solution.py
+++ b/solution.py
@@ -178,13 +178,12 @@
             def _(n=n, dx=dx, dy=dy):
                 halo(n, dx, dy).start()
 
-    for copy in own:
-        copy.wait()
-    for n in range(2):
-        for dx, dy in DIRS:
-            @pl.when(there(-dx, -dy))
-            def _(n=n, dx=dx, dy=dy):
-                halo(n, dx, dy).wait_recv()
+    def arrived(directions):
+        for n in range(2):
+            for dx, dy in directions:
+                @pl.when(there(-dx, -dy))
+                def _(n=n, dx=dx, dy=dy):
+                    halo(n, dx, dy).wait_recv()
 
     row = lax.broadcasted_iota(jnp.int32, (by + 2 * ROWS, bz), 0)
     inside_y = ((row >= ROWS) | (gy > 0)) & ((row < ROWS + by) | (gy < ny - 1))
@@ -195,21 +194,8 @@
 
     inner = slice(ROWS, ROWS + by)
 
-    @pl.loop(1, 2 * RIM + bx - 1)
-    def _(layer):
-        v1[layer] = times_b(v0, dd, layer, inside(layer))
-
-    @pl.loop(2, 2 * RIM + bx - 2)
-    def _(layer):
-        v2[layer] = times_b(v1, dd, layer, inside(layer))
-
-    def tile(a):
-        whole = jnp.sum(a.reshape(by // 8, 8, bz), 0)
-        pad = jnp.concatenate([whole[:, 128:], jnp.zeros((8, 256 - bz), jnp.float32)], 1)
-        return whole[:, :128] + pad
-
-    def body(k, sums):
-        layer = k + RIM
+    def body(layer, sums):
+        k = layer - RIM
         f0 = v0[layer, inner]
         f1 = v1[layer, inner]
         f2 = v2[layer, inner]
@@ -220,7 +206,39 @@
         pairs = (f0 * f0, f0 * f1, f1 * f1, f1 * f2, f2 * f2, f2 * f3)
         return tuple(s + jnp.sum(p.reshape(by // 8, 8, bz), 0) for s, p in zip(sums, pairs))
 
-    sums = lax.fori_loop(0, bx, body, (jnp.zeros((8, bz), jnp.float32),) * 6)
+    def stencils(starts, count, valid, sums):
+        @pl.loop(0, count[0])
+        def _(k):
+            layer = starts[0] + k
+            v1[layer] = times_b(v0, dd, layer, valid(layer))
+
+        @pl.loop(0, count[1])
+        def _(k):
+            layer = starts[1] + k
+            v2[layer] = times_b(v1, dd, layer, valid(layer))
+
+        return lax.fori_loop(0, count[2], lambda k, s: body(starts[2] + k, s), sums)
+
+    for copy in own:
+        copy.wait()
+    arrived(DIRS[2:4])
+    sums = (jnp.zeros((8, bz), jnp.float32),) * 6
+    sums = stencils((RIM + 1, RIM + 2, RIM + 3), (bx - 2, bx - 4, bx - 6), lambda layer: inside_y, sums)
+    near_high = lax.rem(gx, 2) == 0
+    for turn in range(2):
+        high = near_high if turn == 0 else jnp.logical_not(near_high)
+
+        @pl.when(high)
+        def _():
+            arrived([d for d in DIRS if d[0] < 0])
+
+        @pl.when(jnp.logical_not(high))
+        def _():
+            arrived([d for d in DIRS if d[0] > 0])
+
+        starts = tuple(jnp.where(high, RIM + bx - 1 - k, RIM - 2 + k) for k in range(3))
+        sums = stencils(starts, (3, 3, 3), inside, sums)
+
     lane = [jnp.sum(jnp.sum(s, 1, keepdims=True), 0, keepdims=True) for s in sums]
     row8 = lax.broadcasted_iota(jnp.int32, (8, 128), 0)
     packed = jnp.zeros((8, 128), jnp.float32)

time: 30.7 us -> 25.7 us (0.84)
  Pallas kernels: 29.9 us -> 24.9 us
    pallas_call x1, Pallas kernels: 27.9 us -> 22.9 us  [on_device(): pl.pallas_call(functools.partial(kernel, nx, ny), out_shape=(block, block...]
where the time goes in v3:
time: 25.7 us; the launch traced here: 25.6 us
  Pallas kernels  24.9 us (97%)
  between operations  0.65 us (3%)
    pallas_call x1, Pallas kernels, on_device(): pl.pallas_call(functools.partial(kernel, nx, ny), out_shape=(block, block...  22.9 us
    pallas_call x1, Pallas kernels, on_device(): pl.pallas_call(combine, out_shape=(block, block), in_specs=[vmem] * 5, ou...  2.03 us

profile of v3, /device:TPU:0, one launch (start us, length us, event | category | flops | bytes accessed | tf_op | source)
XLA Modules:
  0.0 25.6 jit_solution(13981464673844523886)
XLA Ops:
  0.6 0.0 copy-start
  0.6 22.9 %shard_map.41 = (f32[16,64,192]{2,1,0:T(8,128)S(1)}, f32[16,64,192]{2,1,0:T(8,128)S(1)}, f32[16,64,192]{2,1,0:T(8,128)S(1)}, f32[8,128]{1,0:T(8,128)S(1)}) custom-call(f32[16,64,192]{2,1,0:T(8,128)} %f0_ref.1, f32[16,64,192]{2,1,0:T(8,128)} %d_ref.1), custom_call_target="tpu_custom_call" | custom-call | tf_op jit(solution)/shard_map/pallas_call | solution.py:318
  23.5 0.0 copy-done
  23.5 2.0 %shard_map.42 = (f32[16,64,192]{2,1,0:T(8,128)}, f32[16,64,192]{2,1,0:T(8,128)}) custom-call(f32[16,64,192]{2,1,0:T(8,128)S(1)} %copy-done, f32[16,64,192]{2,1,0:T(8,128)S(1)} %get-tuple-element.6.f1_ref, f32[16,64,192]{2,1,0:T(8,128)S(1)} %get-tuple-element.7.f2_ref, f32[16,64,192]{2,1,0:T(8,128)S(1)} %get-tuple-element.8.f3_ref, ...), custom_call_target="tpu_custom_call" | custom-call | tf_op jit(solution)/shard_map/pallas_call | solution.py:335
Async XLA Ops:
  0.6 22.9 %copy-start = (f32[16,64,192]{2,1,0:T(8,128)S(1)}, f32[16,64,192]{2,1,0:T(8,128)}, u32[]{:S(2)}) copy-start(f32[16,64,192]{2,1,0:T(8,128)} %f0_ref.1) | copy-start | bytes 2359300

commit v4 on v3

--- a/solution.py
+++ b/solution.py
@@ -96,8 +96,8 @@
 
 
 def kernel(nx, ny, b_ref, d_ref, v1_ref, v2_ref, v3_ref, co_ref,
-           v0, dd, v1, v2, part, planes, middle, lines,
-           own_sem, send_sem, recv_sem, px_send, px_recv, py_send, py_recv):
+           v0, dd, v1, v2, part, slots,
+           own_sem, send_sem, recv_sem, sum_send, sum_recv):
     gx, gy = lax.axis_index("gx"), lax.axis_index("gy")
     bx, by, bz = b_ref.shape
     barrier = pltpu.get_barrier_semaphore()
@@ -116,18 +116,16 @@
     def peer_y(k):
         return lax.rem(gy + k, ny)
 
-    for dx, dy in DIRS[4:]:
-        @pl.when(there(dx, dy))
-        def _(dx=dx, dy=dy):
-            pl.semaphore_signal(barrier, inc=1, device_id=(gx + dx, gy + dy), device_id_type=MESH)
-
-    @pl.loop(1, nx)
+    count = nx * ny
+    me = gx * ny + gy
+
+    def peer(k):
+        to = lax.rem(me + k, count)
+        return to // ny, lax.rem(to, ny)
+
+    @pl.loop(1, count)
     def _(k):
-        pl.semaphore_signal(barrier, inc=1, device_id=(peer_x(k), gy), device_id_type=MESH)
-
-    @pl.loop(1, ny)
-    def _(k):
-        pl.semaphore_signal(barrier, inc=1, device_id=(gx, peer_y(k)), device_id_type=MESH)
+        pl.semaphore_signal(barrier, inc=1, device_id=peer(k), device_id_type=MESH)
 
     own = []
     for n, (src, dst) in enumerate(((b_ref, v0), (d_ref, dd))):
@@ -151,15 +149,13 @@
     def _():
         v0[:, ROWS + by:] = jnp.zeros((v0.shape[0], ROWS, bz), jnp.float32)
 
-    expected = nx - 1 + ny - 1
-    for dx, dy in DIRS[4:]:
-        expected = expected + there(dx, dy).astype(jnp.int32)
-    pl.semaphore_wait(barrier, expected)
+    pl.semaphore_wait(barrier, count - 1)
 
     def halo(n, dx, dy):
         width = RIM - n if dx == 0 or dy == 0 else RIM - 1 - n
         width_y = width
-        src, dst = ((b_ref, v0), (d_ref, dd))[n]
+        dst = (v0, dd)[n]
+        src = dst.at[pl.ds(RIM, bx), pl.ds(ROWS, by), :]
         from_x, to_x = span_x(dx, width, bx)
         from_y, to_y = span_y(dy, width_y, by)
         index = DIRS.index((dx, dy))
@@ -172,6 +168,8 @@
             device_id_type=MESH,
         )
 
+    for copy in own:
+        copy.wait()
     for n in range(2):
         for dx, dy in DIRS:
             @pl.when(there(dx, dy))
@@ -219,8 +217,6 @@
 
         return lax.fori_loop(0, count[2], lambda k, s: body(starts[2] + k, s), sums)
 
-    for copy in own:
-        copy.wait()
     arrived(DIRS[2:4])
     sums = (jnp.zeros((8, bz), jnp.float32),) * 6
     sums = stencils((RIM + 1, RIM + 2, RIM + 3), (bx - 2, bx - 4, bx - 6), lambda layer: inside_y, sums)
@@ -240,45 +236,29 @@
         sums = stencils(starts, (3, 3, 3), inside, sums)
 
     lane = [jnp.sum(jnp.sum(s, 1, keepdims=True), 0, keepdims=True) for s in sums]
+    lane_of = lax.broadcasted_iota(jnp.int32, (1, 128), 1)
+    packed = jnp.zeros((1, 128), jnp.float32)
+    for k, s in enumerate(lane):
+        packed = jnp.where(lane_of == k, s, packed)
+    part[0] = packed
+
+    @pl.loop(1, count)
+    def _(k):
+        pltpu.make_async_remote_copy(
+            src_ref=part.at[0], dst_ref=slots.at[me], send_sem=sum_send.at[0],
+            recv_sem=sum_recv.at[0], device_id=peer(k), device_id_type=MESH).start()
+
+    slots[me] = packed
+    others = slots.at[pl.ds(0, count - 1)]
+    pltpu.make_async_copy(others, others, sum_recv.at[0]).wait()
+    total = jnp.sum(slots[...], 0)
+    moments = [total[:, k:k + 1] for k in range(6)]
     row8 = lax.broadcasted_iota(jnp.int32, (8, 128), 0)
-    packed = jnp.zeros((8, 128), jnp.float32)
-    for k, s in enumerate(lane):
-        packed = jnp.where(row8 == k, s, packed)
-    part[...] = packed
-
-    def share(src, slots, k, axis):
-        if axis == 0:
-            mine, target = gx, (peer_x(k), gy)
-            theirs, sems = lax.rem(gx + nx - k, nx), (px_send, px_recv)
-        else:
-            mine, target = gy, (gx, peer_y(k))
-            theirs, sems = lax.rem(gy + ny - k, ny), (py_send, py_recv)
-        return pltpu.make_async_remote_copy(
-            src_ref=src, dst_ref=slots.at[mine], send_sem=sems[0].at[k - 1],
-            recv_sem=sems[1].at[k - 1], device_id=target, device_id_type=MESH)
-
-    def all_sum(src, slots, count, axis):
-        mine = gx if axis == 0 else gy
-
-        @pl.loop(1, count)
-        def _(k):
-            share(src, slots, k, axis).start()
-
-        slots[mine] = src[...]
-
-        @pl.loop(1, count)
-        def _(k):
-            share(src, slots, k, axis).wait()
-
-        return lax.fori_loop(1, count, lambda k, t: t + slots[k], slots[0])
-
-    middle[...] = all_sum(part, planes, nx, 0)
-    total = all_sum(middle, lines, ny, 1)
-    moments = [total[k:k + 1] for k in range(6)]
     co = jnp.zeros((8, 128), jnp.float32)
     for k, c in enumerate(coefficients(moments)):
         co = jnp.where(row8 == k, c, co)
     co_ref[...] = co
+    pltpu.make_async_copy(others, others, sum_send.at[0]).wait()
 
     for n in range(2):
         for dx, dy in DIRS:
@@ -322,12 +302,10 @@
         out_specs=(vmem,) * 4,
         scratch_shapes=[
             big, big, big, big,
-            pltpu.VMEM((8, 128), jnp.float32),
-            pltpu.VMEM((nx, 8, 128), jnp.float32),
-            pltpu.VMEM((8, 128), jnp.float32),
-            pltpu.VMEM((ny, 8, 128), jnp.float32),
+            pltpu.VMEM((1, 1, 128), jnp.float32),
+            pltpu.VMEM((nx * ny, 1, 128), jnp.float32),
             dma((2,)), dma((2, 8)), dma((2, 8)),
-            dma((nx - 1,)), dma((nx - 1,)), dma((ny - 1,)), dma((ny - 1,)),
+            dma((1,)), dma((1,)),
         ],
         compiler_params=pltpu.CompilerParams(
             collective_id=0, has_side_effects=True, vmem_limit_bytes=24 * 2**20),

time: 25.7 us -> 24 us (0.934)
  Pallas kernels: 24.9 us -> 23.2 us
    pallas_call x1, Pallas kernels: 22.9 us -> 21.1 us  [on_device(): pl.pallas_call(functools.partial(kernel, nx, ny), out_shape=(block, block...]
where the time goes in v4:
time: 24 us; the launch traced here: 23.8 us
  Pallas kernels  23.2 us (97%)
  between operations  0.65 us (3%)
    pallas_call x1, Pallas kernels, on_device(): pl.pallas_call(functools.partial(kernel, nx, ny), out_shape=(block, block...  21.1 us
    pallas_call x1, Pallas kernels, on_device(): pl.pallas_call(combine, out_shape=(block, block), in_specs=[vmem] * 5, ou...  2.03 us

profile of v4, /device:TPU:0, one launch (start us, length us, event | category | flops | bytes accessed | tf_op | source)
XLA Modules:
  0.0 23.8 jit_solution(16941385559619147526)
XLA Ops:
  0.6 0.0 copy-start
  0.6 21.1 %shard_map.41 = (f32[16,64,192]{2,1,0:T(8,128)S(1)}, f32[16,64,192]{2,1,0:T(8,128)S(1)}, f32[16,64,192]{2,1,0:T(8,128)S(1)}, f32[8,128]{1,0:T(8,128)S(1)}) custom-call(f32[16,64,192]{2,1,0:T(8,128)} %f0_ref.1, f32[16,64,192]{2,1,0:T(8,128)} %d_ref.1), custom_call_target="tpu_custom_call" | custom-call | tf_op jit(solution)/shard_map/pallas_call | solution.py:298
  21.8 0.0 copy-done
  21.8 2.0 %shard_map.42 = (f32[16,64,192]{2,1,0:T(8,128)}, f32[16,64,192]{2,1,0:T(8,128)}) custom-call(f32[16,64,192]{2,1,0:T(8,128)S(1)} %copy-done, f32[16,64,192]{2,1,0:T(8,128)S(1)} %get-tuple-element.6.f1_ref, f32[16,64,192]{2,1,0:T(8,128)S(1)} %get-tuple-element.7.f2_ref, f32[16,64,192]{2,1,0:T(8,128)S(1)} %get-tuple-element.8.f3_ref, ...), custom_call_target="tpu_custom_call" | custom-call | tf_op jit(solution)/shard_map/pallas_call | solution.py:313
Async XLA Ops:
  0.6 21.2 %copy-start = (f32[16,64,192]{2,1,0:T(8,128)S(1)}, f32[16,64,192]{2,1,0:T(8,128)}, u32[]{:S(2)}) copy-start(f32[16,64,192]{2,1,0:T(8,128)} %f0_ref.1) | copy-start | bytes 2359300

commit v5 on v4

--- a/solution.py
+++ b/solution.py
@@ -31,17 +31,17 @@
     return pl.ds(0, width), pl.ds(ROWS + size, width)
 
 
-def times_b(field, shift, layer, valid):
-    here = field[layer]
+def times_b(field, shift, layer, valid, span=slice(None)):
+    here = field[layer, span]
     rows, lanes = here.shape
     row0 = jnp.zeros((1, lanes), jnp.float32)
     lane0 = jnp.zeros((rows, 1), jnp.float32)
-    beside = field[layer - 1] + field[layer + 1]
+    beside = field[layer - 1, span] + field[layer + 1, span]
     beside = beside + jnp.concatenate([here[1:], row0], 0)
     beside = beside + jnp.concatenate([row0, here[:-1]], 0)
     beside = beside + jnp.concatenate([here[:, 1:], lane0], 1)
     beside = beside + jnp.concatenate([lane0, here[:, :-1]], 1)
-    out = (shift[layer] + (6.0 - SHIFT)) * here - beside
+    out = (shift[layer, span] + (6.0 - SHIFT)) * here - beside
     if valid is None:
         return out
     return jnp.where(valid, out, 0.0)
@@ -97,7 +97,7 @@
 
 def kernel(nx, ny, b_ref, d_ref, v1_ref, v2_ref, v3_ref, co_ref,
            v0, dd, v1, v2, part, slots,
-           own_sem, send_sem, recv_sem, sum_send, sum_recv):
+           tail_out, tail_in, own_sem, send_sem, recv_sem, sum_send, sum_recv, tail_send, tail_recv):
     gx, gy = lax.axis_index("gx"), lax.axis_index("gy")
     bx, by, bz = b_ref.shape
     barrier = pltpu.get_barrier_semaphore()
@@ -148,8 +148,6 @@
     @pl.when(gy == ny - 1)
     def _():
         v0[:, ROWS + by:] = jnp.zeros((v0.shape[0], ROWS, bz), jnp.float32)
-
-    pl.semaphore_wait(barrier, count - 1)
 
     def halo(n, dx, dy):
         width = RIM - n if dx == 0 or dy == 0 else RIM - 1 - n
@@ -159,9 +157,10 @@
         from_x, to_x = span_x(dx, width, bx)
         from_y, to_y = span_y(dy, width_y, by)
         index = DIRS.index((dx, dy))
+        lanes = pl.ds(0, bz // 128 * 128) if dy == 0 else slice(None)
         return pltpu.make_async_remote_copy(
-            src_ref=src.at[from_x, from_y, :],
-            dst_ref=dst.at[to_x, to_y, :],
+            src_ref=src.at[from_x, from_y, lanes],
+            dst_ref=dst.at[to_x, to_y, lanes],
             send_sem=send_sem.at[n, index],
             recv_sem=recv_sem.at[n, index],
             device_id=(gx + dx, gy + dy),
@@ -170,11 +169,53 @@
 
     for copy in own:
         copy.wait()
+    full = bz // 128 * 128
+    tail = bz - full
+    half = by // 2
+    last = pl.ds(full, tail)
+
+    def tails(dx, sending):
+        first, second = pl.ds(0, tail), pl.ds(tail, tail)
+        low = {(True, 1): RIM + bx - 1, (True, -1): RIM, (False, 1): RIM - 1,
+               (False, -1): RIM + bx}[sending, dx]
+        at = [low - dx * k for k in range(RIM)]
+        every = pl.ds(ROWS, by)
+        return (
+            (v0, at[0], every, pl.ds(0, by), first),
+            (v0, at[1], every, pl.ds(0, by), second),
+            (v0, at[2], every, pl.ds(by, by), first),
+            (dd, at[0], every, pl.ds(by, by), second),
+            (dd, at[1], pl.ds(ROWS, half), pl.ds(2 * by, half), first),
+            (dd, at[1], pl.ds(ROWS + half, half), pl.ds(2 * by, half), second),
+        )
+
+    for side, dx in enumerate((1, -1)):
+        for array, layer, rows, to, lanes in tails(dx, True):
+            tail_out[side, to, lanes] = array[layer, rows, last]
+
+    def tail_copy(dx):
+        side = (1, -1).index(dx)
+        return pltpu.make_async_remote_copy(
+            src_ref=tail_out.at[side], dst_ref=tail_in.at[side], send_sem=tail_send.at[side],
+            recv_sem=tail_recv.at[side], device_id=(gx + dx, gy), device_id_type=MESH)
+
+    def unpack(dx):
+        side = (1, -1).index(dx)
+        for array, layer, rows, to, lanes in tails(dx, False):
+            array[layer, rows, last] = tail_in[side, to, lanes]
+
+    pl.semaphore_wait(barrier, count - 1)
+
     for n in range(2):
         for dx, dy in DIRS:
             @pl.when(there(dx, dy))
             def _(n=n, dx=dx, dy=dy):
                 halo(n, dx, dy).start()
+
+    for dx in (1, -1):
+        @pl.when(there(dx, 0))
+        def _(dx=dx):
+            tail_copy(dx).start()
 
     def arrived(directions):
         for n in range(2):
@@ -192,17 +233,19 @@
 
     inner = slice(ROWS, ROWS + by)
 
+    def add_up(layer, span, f3, sums):
+        k = layer - RIM
+        rows = slice(span.start - ROWS, span.stop - ROWS)
+        f0, f1, f2 = v0[layer, span], v1[layer, span], v2[layer, span]
+        v1_ref[k, rows] = f1
+        v2_ref[k, rows] = f2
+        v3_ref[k, rows] = f3
+        pairs = (f0 * f0, f0 * f1, f1 * f1, f1 * f2, f2 * f2, f2 * f3)
+        groups = (span.stop - span.start) // 8
+        return tuple(s + jnp.sum(p.reshape(groups, 8, bz), 0) for s, p in zip(sums, pairs))
+
     def body(layer, sums):
-        k = layer - RIM
-        f0 = v0[layer, inner]
-        f1 = v1[layer, inner]
-        f2 = v2[layer, inner]
-        f3 = times_b(v2, dd, layer, None)[inner]
-        v1_ref[k] = f1
-        v2_ref[k] = f2
-        v3_ref[k] = f3
-        pairs = (f0 * f0, f0 * f1, f1 * f1, f1 * f2, f2 * f2, f2 * f3)
-        return tuple(s + jnp.sum(p.reshape(by // 8, 8, bz), 0) for s, p in zip(sums, pairs))
+        return add_up(layer, inner, times_b(v2, dd, layer, None)[inner], sums)
 
     def stencils(starts, count, valid, sums):
         @pl.loop(0, count[0])
@@ -217,9 +260,50 @@
 
         return lax.fori_loop(0, count[2], lambda k, s: body(starts[2] + k, s), sums)
 
+    sums = (jnp.zeros((8, bz), jnp.float32),) * 6
+
+    @pl.loop(RIM + 1, RIM + bx - 1)
+    def _(layer):
+        v1[layer, inner] = times_b(v0, dd, layer, None, inner)
+
+    @pl.loop(RIM + 2, RIM + bx - 2)
+    def _(layer):
+        v2[layer, inner] = times_b(v1, dd, layer, None, inner)
+
+    middle = slice(2 * ROWS, by)
+
+    def middle_rows(layer, sums):
+        f3 = times_b(v2, dd, layer, None, inner)[ROWS:by - ROWS]
+        return add_up(layer, middle, f3, sums)
+
+    sums = lax.fori_loop(RIM + 3, RIM + bx - 3, middle_rows, sums)
+
     arrived(DIRS[2:4])
-    sums = (jnp.zeros((8, bz), jnp.float32),) * 6
-    sums = stencils((RIM + 1, RIM + 2, RIM + 3), (bx - 2, bx - 4, bx - 6), lambda layer: inside_y, sums)
+    low_rows, high_rows = slice(0, 3 * ROWS), slice(by - ROWS, by + 2 * ROWS)
+    low_in, high_in = gy > 0, gy < ny - 1
+    short = lax.broadcasted_iota(jnp.int32, (3 * ROWS, bz), 0)
+    low_ok = (short >= ROWS) | low_in
+    high_ok = (short < 2 * ROWS) | high_in
+
+    def ends(field, out, layer):
+        out[layer, 0:2 * ROWS] = times_b(field, dd, layer, low_ok, low_rows)[:2 * ROWS]
+        out[layer, by:by + 2 * ROWS] = times_b(field, dd, layer, high_ok, high_rows)[ROWS:]
+
+    @pl.loop(RIM + 1, RIM + bx - 1)
+    def _(layer):
+        ends(v0, v1, layer)
+
+    @pl.loop(RIM + 2, RIM + bx - 2)
+    def _(layer):
+        ends(v1, v2, layer)
+
+    def end_rows(layer, sums):
+        f3 = times_b(v2, dd, layer, None, low_rows)[ROWS:2 * ROWS]
+        sums = add_up(layer, slice(ROWS, 2 * ROWS), f3, sums)
+        f3 = times_b(v2, dd, layer, None, high_rows)[ROWS:2 * ROWS]
+        return add_up(layer, slice(by, by + ROWS), f3, sums)
+
+    sums = lax.fori_loop(RIM + 3, RIM + bx - 3, end_rows, sums)
     near_high = lax.rem(gx, 2) == 0
     for turn in range(2):
         high = near_high if turn == 0 else jnp.logical_not(near_high)
@@ -228,9 +312,19 @@
         def _():
             arrived([d for d in DIRS if d[0] < 0])
 
+            @pl.when(there(1, 0))
+            def _():
+                tail_copy(-1).wait_recv()
+                unpack(-1)
+
         @pl.when(jnp.logical_not(high))
         def _():
             arrived([d for d in DIRS if d[0] > 0])
+
+            @pl.when(there(-1, 0))
+            def _():
+                tail_copy(1).wait_recv()
+                unpack(1)
 
         starts = tuple(jnp.where(high, RIM + bx - 1 - k, RIM - 2 + k) for k in range(3))
         sums = stencils(starts, (3, 3, 3), inside, sums)
@@ -265,6 +359,11 @@
             @pl.when(there(dx, dy))
             def _(n=n, dx=dx, dy=dy):
                 halo(n, dx, dy).wait_send()
+
+    for dx in (1, -1):
+        @pl.when(there(dx, 0))
+        def _(dx=dx):
+            tail_copy(dx).wait_send()
 
 
 def combine(f0_ref, f1_ref, f2_ref, f3_ref, co_ref, x_ref, r_ref, x_out, r_out, sems):
@@ -304,8 +403,10 @@
             big, big, big, big,
             pltpu.VMEM((1, 1, 128), jnp.float32),
             pltpu.VMEM((nx * ny, 1, 128), jnp.float32),
+            pltpu.VMEM((2, 2 * by + by // 2, 128), jnp.float32),
+            pltpu.VMEM((2, 2 * by + by // 2, 128), jnp.float32),
             dma((2,)), dma((2, 8)), dma((2, 8)),
-            dma((1,)), dma((1,)),
+            dma((1,)), dma((1,)), dma((2,)), dma((2,)),
         ],
         compiler_params=pltpu.CompilerParams(
             collective_id=0, has_side_effects=True, vmem_limit_bytes=24 * 2**20),

time: 24 us -> 23.5 us (0.979)
  Pallas kernels: 23.2 us -> 22.7 us
    pallas_call x1, Pallas kernels: 21.1 us -> 20.7 us  [on_device(): pl.pallas_call(functools.partial(kernel, nx, ny), out_shape=(block, block...]
where the time goes in v5:
time: 23.5 us; the launch traced here: 23.4 us
  Pallas kernels  22.7 us (97%)
  between operations  0.65 us (3%)
    pallas_call x1, Pallas kernels, on_device(): pl.pallas_call(functools.partial(kernel, nx, ny), out_shape=(block, block...  20.7 us
    pallas_call x1, Pallas kernels, on_device(): pl.pallas_call(combine, out_shape=(block, block), in_specs=[vmem] * 5, ou...  2.03 us

profile of v5, /device:TPU:0, one launch (start us, length us, event | category | flops | bytes accessed | tf_op | source)
XLA Modules:
  0.0 23.4 jit_solution(13219275503860021502)
XLA Ops:
  0.6 0.0 copy-start
  0.6 20.7 %shard_map.41 = (f32[16,64,192]{2,1,0:T(8,128)S(1)}, f32[16,64,192]{2,1,0:T(8,128)S(1)}, f32[16,64,192]{2,1,0:T(8,128)S(1)}, f32[8,128]{1,0:T(8,128)S(1)}) custom-call(f32[16,64,192]{2,1,0:T(8,128)} %f0_ref.1, f32[16,64,192]{2,1,0:T(8,128)} %d_ref.1), custom_call_target="tpu_custom_call" | custom-call | tf_op jit(solution)/shard_map/pallas_call | solution.py:397
  21.3 0.0 copy-done
  21.3 2.0 %shard_map.42 = (f32[16,64,192]{2,1,0:T(8,128)}, f32[16,64,192]{2,1,0:T(8,128)}) custom-call(f32[16,64,192]{2,1,0:T(8,128)S(1)} %copy-done, f32[16,64,192]{2,1,0:T(8,128)S(1)} %get-tuple-element.6.f1_ref, f32[16,64,192]{2,1,0:T(8,128)S(1)} %get-tuple-element.7.f2_ref, f32[16,64,192]{2,1,0:T(8,128)S(1)} %get-tuple-element.8.f3_ref, ...), custom_call_target="tpu_custom_call" | custom-call | tf_op jit(solution)/shard_map/pallas_call | solution.py:414
Async XLA Ops:
  0.6 20.7 %copy-start = (f32[16,64,192]{2,1,0:T(8,128)S(1)}, f32[16,64,192]{2,1,0:T(8,128)}, u32[]{:S(2)}) copy-start(f32[16,64,192]{2,1,0:T(8,128)} %f0_ref.1) | copy-start | bytes 2359300

commit v6 on v5

--- a/solution.py
+++ b/solution.py
@@ -248,25 +248,25 @@
         return add_up(layer, inner, times_b(v2, dd, layer, None)[inner], sums)
 
     def stencils(starts, count, valid, sums):
-        @pl.loop(0, count[0])
+        @pl.loop(0, count[0], unroll=True)
         def _(k):
             layer = starts[0] + k
             v1[layer] = times_b(v0, dd, layer, valid(layer))
 
-        @pl.loop(0, count[1])
+        @pl.loop(0, count[1], unroll=True)
         def _(k):
             layer = starts[1] + k
             v2[layer] = times_b(v1, dd, layer, valid(layer))
 
-        return lax.fori_loop(0, count[2], lambda k, s: body(starts[2] + k, s), sums)
+        return lax.fori_loop(0, count[2], lambda k, s: body(starts[2] + k, s), sums, unroll=True)
 
     sums = (jnp.zeros((8, bz), jnp.float32),) * 6
 
-    @pl.loop(RIM + 1, RIM + bx - 1)
+    @pl.loop(RIM + 1, RIM + bx - 1, unroll=2)
     def _(layer):
         v1[layer, inner] = times_b(v0, dd, layer, None, inner)
 
-    @pl.loop(RIM + 2, RIM + bx - 2)
+    @pl.loop(RIM + 2, RIM + bx - 2, unroll=2)
     def _(layer):
         v2[layer, inner] = times_b(v1, dd, layer, None, inner)
 
@@ -276,7 +276,7 @@
         f3 = times_b(v2, dd, layer, None, inner)[ROWS:by - ROWS]
         return add_up(layer, middle, f3, sums)
 
-    sums = lax.fori_loop(RIM + 3, RIM + bx - 3, middle_rows, sums)
+    sums = lax.fori_loop(RIM + 3, RIM + bx - 3, middle_rows, sums, unroll=2)
 
     arrived(DIRS[2:4])
     low_rows, high_rows = slice(0, 3 * ROWS), slice(by - ROWS, by + 2 * ROWS)
@@ -289,11 +289,11 @@
         out[layer, 0:2 * ROWS] = times_b(field, dd, layer, low_ok, low_rows)[:2 * ROWS]
         out[layer, by:by + 2 * ROWS] = times_b(field, dd, layer, high_ok, high_rows)[ROWS:]
 
-    @pl.loop(RIM + 1, RIM + bx - 1)
+    @pl.loop(RIM + 1, RIM + bx - 1, unroll=2)
     def _(layer):
         ends(v0, v1, layer)
 
-    @pl.loop(RIM + 2, RIM + bx - 2)
+    @pl.loop(RIM + 2, RIM + bx - 2, unroll=2)
     def _(layer):
         ends(v1, v2, layer)
 
@@ -303,7 +303,7 @@
         f3 = times_b(v2, dd, layer, None, high_rows)[ROWS:2 * ROWS]
         return add_up(layer, slice(by, by + ROWS), f3, sums)
 
-    sums = lax.fori_loop(RIM + 3, RIM + bx - 3, end_rows, sums)
+    sums = lax.fori_loop(RIM + 3, RIM + bx - 3, end_rows, sums, unroll=2)
     near_high = lax.rem(gx, 2) == 0
     for turn in range(2):
         high = near_high if turn == 0 else jnp.logical_not(near_high)

time: 23.5 us -> 21.5 us (0.915)
  Pallas kernels: 22.7 us -> 20.7 us
    pallas_call x1, Pallas kernels: 20.7 us -> 18.7 us  [on_device(): pl.pallas_call(functools.partial(kernel, nx, ny), out_shape=(block, block...]
where the time goes in v6:
time: 21.5 us; the launch traced here: 21.4 us
  Pallas kernels  20.7 us (96%)
  between operations  0.65 us (3%)
    pallas_call x1, Pallas kernels, on_device(): pl.pallas_call(functools.partial(kernel, nx, ny), out_shape=(block, block...  18.7 us
    pallas_call x1, Pallas kernels, on_device(): pl.pallas_call(combine, out_shape=(block, block), in_specs=[vmem] * 5, ou...  2.03 us

profile of v6, /device:TPU:0, one launch (start us, length us, event | category | flops | bytes accessed | tf_op | source)
XLA Modules:
  0.0 21.4 jit_solution(9867865796342531743)
XLA Ops:
  0.6 0.0 copy-start
  0.6 18.7 %shard_map.41 = (f32[16,64,192]{2,1,0:T(8,128)S(1)}, f32[16,64,192]{2,1,0:T(8,128)S(1)}, f32[16,64,192]{2,1,0:T(8,128)S(1)}, f32[8,128]{1,0:T(8,128)S(1)}) custom-call(f32[16,64,192]{2,1,0:T(8,128)} %f0_ref.1, f32[16,64,192]{2,1,0:T(8,128)} %d_ref.1), custom_call_target="tpu_custom_call" | custom-call | tf_op jit(solution)/shard_map/pallas_call | solution.py:397
  19.3 0.0 copy-done
  19.4 2.0 %shard_map.42 = (f32[16,64,192]{2,1,0:T(8,128)}, f32[16,64,192]{2,1,0:T(8,128)}) custom-call(f32[16,64,192]{2,1,0:T(8,128)S(1)} %copy-done, f32[16,64,192]{2,1,0:T(8,128)S(1)} %get-tuple-element.6.f1_ref, f32[16,64,192]{2,1,0:T(8,128)S(1)} %get-tuple-element.7.f2_ref, f32[16,64,192]{2,1,0:T(8,128)S(1)} %get-tuple-element.8.f3_ref, ...), custom_call_target="tpu_custom_call" | custom-call | tf_op jit(solution)/shard_map/pallas_call | solution.py:414
Async XLA Ops:
  0.6 18.7 %copy-start = (f32[16,64,192]{2,1,0:T(8,128)S(1)}, f32[16,64,192]{2,1,0:T(8,128)}, u32[]{:S(2)}) copy-start(f32[16,64,192]{2,1,0:T(8,128)} %f0_ref.1) | copy-start | bytes 2359300
